TPU v7x, 32 devices: a whole 2x2x4 slice. The times are simulated.
32 devices in a mesh: expert: 4 (over y, x), shard: 8 (over z, core).
Axes of the slice: x: 2, y: 2, z: 4, core: 2. Of those that a mesh axis runs over, the one named last changes fastest.
Arguments:
- master_gate: float32 [64, 2048, 1408], P('expert', 'shard'), may hold values from -0.1875 to 0.1875
- master_up: float32 [64, 2048, 1408], P('expert', 'shard'), may hold values from -0.1875 to 0.1875
- master_down: float32 [64, 1408, 2048], P('expert', None, 'shard'), may hold values from -0.21875 to 0.21875
- router_weight: float32 [2048, 64], P('shard', 'expert'), may hold values from -0.125 to 0.125
- router_gain: float32 [2048], P('shard'), may hold values from 0.25 to 1.75
Outputs:
- final_gate: bfloat16 [64, 2048, 1408], P('expert', None, 'shard')
- final_up: bfloat16 [64, 2048, 1408], P('expert', None, 'shard')
- final_down: bfloat16 [64, 1408, 2048], P('expert', 'shard')
- scale_gate: float32 [64, 1408], P('expert', 'shard')
- scale_up: float32 [64, 1408], P('expert', 'shard')
- scale_down: float32 [64, 1408], P('expert', 'shard')
- serve_router: bfloat16 [2048, 64], replicated
All inputs are finite; a program needn't handle non-finite values. Where the computation divides by a largest or mean magnitude, that divisor is 1e-20 or more.
Results may differ from a plain program's by a relative error of at most 0.001.
Values may be sent and summed in bfloat16 or wider, within the bound.
A program may use at most 256 MiB of HBM per device.

v0:
```python
import jax
import jax.numpy as jnp
from jax import lax
from jax.sharding import PartitionSpec as P


def body(master_gate, master_up, master_down, router_weight, router_gain):
    scale_gate, scale_up, scale_down = lax.pmax(
        (
            jnp.max(jnp.abs(master_gate), axis=1),
            jnp.max(jnp.abs(master_up), axis=1),
            jnp.max(jnp.abs(master_down), axis=2),
        ),
        "shard",
    )
    narrow_gate, narrow_up, narrow_down = (
        (master_gate / jnp.expand_dims(scale_gate, 1)).astype(jnp.bfloat16),
        (master_up / jnp.expand_dims(scale_up, 1)).astype(jnp.bfloat16),
        (master_down / jnp.expand_dims(scale_down, 2)).astype(jnp.bfloat16),
    )
    final_gate, final_up = (
        lax.all_to_all(narrow_gate, "shard", split_axis=2, concat_axis=1, tiled=True),
        lax.all_to_all(narrow_up, "shard", split_axis=2, concat_axis=1, tiled=True),
    )
    final_down = lax.all_to_all(narrow_down, "shard", split_axis=1, concat_axis=2, tiled=True)
    scale_gate = lax.dynamic_slice_in_dim(
        scale_gate, lax.axis_index("shard") * final_gate.shape[2], final_gate.shape[2], axis=1
    )
    scale_up = lax.dynamic_slice_in_dim(
        scale_up, lax.axis_index("shard") * final_up.shape[2], final_up.shape[2], axis=1
    )
    scale_down = lax.dynamic_slice_in_dim(
        scale_down, lax.axis_index("shard") * final_down.shape[1], final_down.shape[1], axis=1
    )
    part_router = (router_weight * router_gain[:, None]).astype(jnp.bfloat16)
    row_router = lax.all_gather(part_router, "shard", axis=0, tiled=True)
    serve_router = lax.all_gather(row_router, "expert", axis=1, tiled=True)
    return (final_gate, final_up, final_down, scale_gate, scale_up, scale_down, serve_router)


def solution(mesh):
    return jax.shard_map(
        body,
        mesh=mesh,
        in_specs=(
            P("expert", "shard", None),
            P("expert", "shard", None),
            P("expert", None, "shard"),
            P("shard", "expert"),
            P("shard"),
        ),
        out_specs=(
            P("expert", None, "shard"),
            P("expert", None, "shard"),
            P("expert", "shard", None),
            P("expert", "shard"),
            P("expert", "shard"),
            P("expert", "shard"),
            P(),
        ),
        check_vma=False,
    )
```

profile of v0, /device:TPU:0, one launch (start us, length us, event | category | flops | bytes accessed | tf_op | source)
XLA Modules:
  0.0 985.2 jit_solution(7565016768209817902)
XLA Ops:
  7.2 0.0 all-reduce.3.cloned.1.call-start
  7.2 0.0 slice-start
  7.2 0.0 slice-start.1
  7.2 0.0 slice-start.2
  7.2 10.5 %abs_reduce_fusion = f32[16,1408]{1,0:T(8,128)} fusion(f32[16,1408,256]{2,1,0:T(8,128)} %param.7), kind=kLoop, calls=%fused_computation.2 | loop fusion | flops 11511808 | bytes 23158784 | tf_op jit(solution)/shard_map/reduce_max | solution.py:12
  17.7 0.0 slice-start.3
  17.7 10.8 %abs_reduce_fusion.1 = f32[16,1408]{1,0:T(8,128)} fusion(f32[16,256,1408]{2,1,0:T(8,128)} %param.6), kind=kLoop, calls=%fused_computation.4 | loop fusion | flops 11511808 | bytes 23158784 | tf_op jit(solution)/shard_map/reduce_max | solution.py:11
  28.5 0.0 slice-done
  28.5 0.0 slice-done.1
  28.6 0.0 slice-done.2
  28.6 0.0 slice-done.3
  28.6 0.0 slice-done.4
  28.6 0.0 slice-done.5
  28.6 2.4 abs_reduce_fusion.2
  31.0 0.0 all-reduce.3.cloned.1.call-update
  31.0 23.7 %copy.24 = f32[16,256,1408]{1,0,2:T(8,128)} copy(f32[16,256,1408]{2,1,0:T(8,128)} %param.5) | data formatting | bytes 46137344 | tf_op args[0]
  54.7 32.5 %all-reduce.3.cloned.1.call-done = (f32[16,1408]{1,0:T(8,128)}, f32[16,1408]{1,0:T(8,128)}, f32[16,1408]{1,0:T(8,128)}) async-done(((f32[16,1408]{1,0:T(8,128)}, f32[16,1408]{1,0:T(8,128)}, f32[16,1408]{1,0:T(8,128)}), (f32[16,1408]{1,0:T(8,128)}, f32[16,1408]{1,0:T(8,128)}, f32[16,1408]{1,0:T(8,128)})) %all-reduce.3.cloned.1.call-update) | async-done | bytes 270352 | tf_op jit(solution)/shard_map/pmax | solution.py:8
  87.2 1.1 copy.23
  88.4 14.2 %divide_convert_fusion.1 = bf16[16,256,1408]{1,0,2:T(8,128)(2,1)} fusion(f32[16,256,1408]{1,0,2:T(8,128)} %copy.24, f32[16,1408]{0,1:T(8,128)S(1)} %copy.23), kind=kLoop, calls=%fused_computation.5 | loop fusion | flops 11534336 | bytes 34693120 | tf_op jit(solution)/shard_map/convert_element_type | solution.py:17
  102.6 5.4 all-to-all-start
  108.0 23.7 %copy.28 = f32[16,256,1408]{1,0,2:T(8,128)} copy(f32[16,256,1408]{2,1,0:T(8,128)} %param.6) | data formatting | bytes 46137344 | tf_op args[1]
  131.7 0.0 copy-done
  131.7 0.3 copy.27
  132.0 0.0 copy-start.1
  132.0 14.2 %divide_convert_fusion = bf16[16,256,1408]{1,0,2:T(8,128)(2,1)} fusion(f32[16,256,1408]{1,0,2:T(8,128)} %copy.28, f32[16,1408]{0,1:T(8,128)S(1)} %copy.27), kind=kLoop, calls=%fused_computation.3 | loop fusion | flops 11534336 | bytes 34693120 | tf_op jit(solution)/shard_map/convert_element_type | solution.py:18
  146.2 213.1 %all-to-all-done = bf16[16,256,1408]{1,0,2:T(8,128)(2,1)} async-done(((bf16[16,256,1408]{1,0,2:T(8,128)(2,1)}), bf16[16,256,1408]{1,0,2:T(8,128)(2,1)}, u32[]{:S(2)}, u32[]{:S(2)}) %all-to-all-start) | async-done | bytes 11534368 | tf_op jit(solution)/shard_map/all_to_all | solution.py:22
  359.4 5.2 all-to-all-start.1
  364.6 0.0 copy-done.1
  364.6 0.3 copy.31
  364.9 0.0 copy-start.2
  364.9 0.0 copy-start.3
  364.9 32.6 %fusion = bf16[16,1408,256]{2,0,1:T(8,128)(2,1)} fusion(f32[16,1408,256]{2,1,0:T(8,128)} %param.7, f32[16,1408]{0,1:T(8,128)S(1)} %copy.31), kind=kLoop, calls=%fused_computation.1 | loop fusion | flops 11534336 | bytes 34693120 | tf_op jit(solution)/shard_map/convert_element_type | solution.py:19
  397.5 218.4 %all-to-all-done.1 = bf16[16,256,1408]{1,0,2:T(8,128)(2,1)} async-done(((bf16[16,256,1408]{1,0,2:T(8,128)(2,1)}), bf16[16,256,1408]{1,0,2:T(8,128)(2,1)}, u32[]{:S(2)}, u32[]{:S(2)}) %all-to-all-start.1) | async-done | bytes 11534368 | tf_op jit(solution)/shard_map/all_to_all | solution.py:23
  615.9 5.3 all-to-all-start.2
  621.2 0.0 copy-done.2
  621.2 0.0 copy-done.3
  621.3 257.3 %all_gather.6 = bf16[2048,16]{0,1:T(8,128)(2,1)S(1)} all-gather(bf16[256,16]{0,1:T(8,128)(2,1)S(1)} %multiply_convert_fusion), channel_id=1, replica_groups=mesh['expert'=4,'shard'=8] {'shard'}, dimensions={0}, use_global_device_ids=true | all-gather | bytes 73728 | tf_op jit(solution)/shard_map/all_gather | solution.py:36
  878.5 9.1 all_gather.7
  887.7 1.4 constant_dynamic-slice_fusion.2
  889.1 0.7 constant_dynamic-slice_fusion
  889.8 11.3 %copy.26 = bf16[16,8,256,176]{2,1,3,0:T(8,128)(2,1)} copy(bf16[16,8,256,176]{2,0,3,1:T(8,128)(2,1)} %bitcast.2) | data formatting | bytes 23068672 | tf_op jit(solution)/shard_map/all_to_all | solution.py:22
  901.1 18.0 %all_to_all.42 = bf16[16,2048,176]{1,2,0:T(8,128)(2,1)} reshape(bf16[16,8,256,176]{2,1,3,0:T(8,128)(2,1)} %copy.26) | data formatting | bytes 23068672 | tf_op jit(solution)/shard_map/all_to_all | solution.py:22
  919.1 11.3 %copy.30 = bf16[16,8,256,176]{2,1,3,0:T(8,128)(2,1)} copy(bf16[16,8,256,176]{2,0,3,1:T(8,128)(2,1)} %bitcast.5) | data formatting | bytes 23068672 | tf_op jit(solution)/shard_map/all_to_all | solution.py:23
  930.4 18.0 %all_to_all.46 = bf16[16,2048,176]{1,2,0:T(8,128)(2,1)} reshape(bf16[16,8,256,176]{2,1,3,0:T(8,128)(2,1)} %copy.30) | data formatting | bytes 23068672 | tf_op jit(solution)/shard_map/all_to_all | solution.py:23
  948.4 0.0 all-to-all-done.2
  948.4 11.4 %copy.33 = bf16[16,176,8,256]{3,2,1,0:T(8,128)(2,1)} copy(bf16[16,176,8,256]{3,0,1,2:T(8,128)(2,1)} %bitcast.7) | data formatting | bytes 23068672 | tf_op jit(solution)/shard_map/all_to_all | solution.py:25
  959.7 18.0 %all_to_all.50 = bf16[16,176,2048]{2,1,0:T(8,128)(2,1)} reshape(bf16[16,176,8,256]{3,2,1,0:T(8,128)(2,1)} %copy.33) | data formatting | bytes 23068672 | tf_op jit(solution)/shard_map/all_to_all | solution.py:25
  977.7 0.7 copy.43
  (5 shorter events, 0.0 us)
Async XLA Ops:
  7.2 80.1 %all-reduce.3.cloned.1.call-start = ((), (), s32[]{:S(2)}) async-start(), calls=%async_computation.3 | async-start | bytes 540672 | tf_op jit(solution)/shard_map/pmax | solution.py:8
  7.2 21.3 %slice-start = ((s8[23068672]{0:T(1024)(128)(4,1)}), s8[4194304]{0:T(1024)(128)(4,1)S(1)}, s32[]{:S(2)}) async-start(s8[23068672]{0:T(1024)(128)(4,1)} %bitcast.19), calls=%async_computation.4 | async-start | bytes 8388608
  7.2 21.3 %slice-start.1 = ((s8[23068672]{0:T(1024)(128)(4,1)}), s8[4194304]{0:T(1024)(128)(4,1)S(1)}, s32[]{:S(2)}) async-start(s8[23068672]{0:T(1024)(128)(4,1)} %bitcast.19), calls=%async_computation.5 | async-start | bytes 8388608
  7.2 21.3 %slice-start.2 = ((s8[23068672]{0:T(1024)(128)(4,1)}), s8[4194304]{0:T(1024)(128)(4,1)S(1)}, s32[]{:S(2)}) async-start(s8[23068672]{0:T(1024)(128)(4,1)} %bitcast.19), calls=%async_computation.6 | async-start | bytes 8388608
  17.7 10.8 %slice-start.3 = ((s8[23068672]{0:T(1024)(128)(4,1)}), s8[4194304]{0:T(1024)(128)(4,1)S(1)}, s32[]{:S(2)}) async-start(s8[23068672]{0:T(1024)(128)(4,1)} %bitcast.19), calls=%async_computation.7 | async-start | bytes 8388608
  17.7 10.8 %slice-start.4 = ((s8[23068672]{0:T(1024)(128)(4,1)}), s8[4194304]{0:T(1024)(128)(4,1)S(1)}, s32[]{:S(2)}) async-start(s8[23068672]{0:T(1024)(128)(4,1)} %bitcast.19), calls=%async_computation.8 | async-start | bytes 8388608
  17.7 10.9 %slice-start.5 = ((s8[23068672]{0:T(1024)(128)(4,1)}), s8[2097152]{0:T(1024)(128)(4,1)S(1)}, s32[]{:S(2)}) async-start(s8[23068672]{0:T(1024)(128)(4,1)} %bitcast.19), calls=%async_computation.9 | async-start | bytes 4194304
  102.6 256.8 %all-to-all-start = ((bf16[16,256,1408]{1,0,2:T(8,128)(2,1)}), bf16[16,256,1408]{1,0,2:T(8,128)(2,1)}, u32[]{:S(2)}, u32[]{:S(2)}) async-start(bf16[16,256,1408]{1,0,2:T(8,128)(2,1)} %divide_convert_fusion.1), calls=%async_computation | async-start | bytes 23068672 | tf_op jit(solution)/shard_map/all_to_all | solution.py:22
  108.0 23.7 %copy-start = (f32[16,1408]{1,0:T(8,128)S(1)}, f32[16,1408]{1,0:T(8,128)}, u32[]{:S(2)}) copy-start(f32[16,1408]{1,0:T(8,128)} %get-tuple-element.8) | copy-start | bytes 270340
  132.0 232.6 %copy-start.1 = (f32[16,1408]{1,0:T(8,128)S(1)}, f32[16,1408]{1,0:T(8,128)}, u32[]{:S(2)}) copy-start(f32[16,1408]{1,0:T(8,128)} %get-tuple-element.9) | copy-start | bytes 270340
  359.4 256.5 %all-to-all-start.1 = ((bf16[16,256,1408]{1,0,2:T(8,128)(2,1)}), bf16[16,256,1408]{1,0,2:T(8,128)(2,1)}, u32[]{:S(2)}, u32[]{:S(2)}) async-start(bf16[16,256,1408]{1,0,2:T(8,128)(2,1)} %divide_convert_fusion), calls=%async_computation.1 | async-start | bytes 23068672 | tf_op jit(solution)/shard_map/all_to_all | solution.py:23
  364.9 256.3 %copy-start.2 = (f32[256,16]{0,1:T(8,128)S(1)}, f32[256,16]{0,1:T(8,128)}, u32[]{:S(2)}) copy-start(f32[256,16]{0,1:T(8,128)} %param.8) | copy-start | bytes 49156
  364.9 256.3 %copy-start.3 = (f32[256]{0:T(256)S(1)}, f32[256]{0:T(256)}, u32[]{:S(2)}) copy-start(f32[256]{0:T(256)} %param.9) | copy-start | bytes 3076
  615.9 332.5 %all-to-all-start.2 = ((bf16[16,1408,256]{2,0,1:T(8,128)(2,1)}), bf16[16,1408,256]{2,0,1:T(8,128)(2,1)}, u32[]{:S(2)}, u32[]{:S(2)}) async-start(bf16[16,1408,256]{2,0,1:T(8,128)(2,1)} %fusion), calls=%async_computation.2 | async-start | bytes 23068672 | tf_op jit(solution)/shard_map/all_to_all | solution.py:25
Sparse Core Ops, SparseCore 0:
  31.1 56.0 all-reduce.2
where the time goes:
time: 988 us; the launch traced here: 985 us
  waiting for transfers between devices  464 us (47%)
  blocking collectives  266 us (27%)
  local copies, waits for them, and re-layouts  140 us (14%)
  other arithmetic  84.8 us (9%)
  starting transfers between devices  16 us (2%)
  between operations  14.2 us (1%)
    all_gather x1, blocking collectives, body(): row_router = lax.all_gather(part_router, 'shard', axis=0, tiled=True)  257 us
    all_to_all x1, waiting for transfers between devices, body(): lax.all_to_all(narrow_up, 'shard', split_axis=2, concat_axis=1, tiled=True)  218 us
    all_to_all x1, waiting for transfers between devices, body(): lax.all_to_all(narrow_gate, 'shard', split_axis=2, concat_axis=1, tiled=T...  213 us
    unnamed x23, local copies, waits for them, and re-layouts  48.2 us
    convert_element_type x1, other arithmetic, body(): (master_down / jnp.expand_dims(scale_down, 2)).astype(jnp.bfloat16)  32.6 us
    pmax x1, waiting for transfers between devices, body(): lax.pmax((jnp.max(jnp.abs(master_gate), axis=1), jnp.max(jnp.abs(master_u...  32.5 us
    all_to_all x2, local copies, waits for them, and re-layouts, body(): lax.all_to_all(narrow_down, 'shard', split_axis=1, concat_axis=2, tiled=T...  29.3 us
    all_to_all x2, local copies, waits for them, and re-layouts, body(): lax.all_to_all(narrow_gate, 'shard', split_axis=2, concat_axis=1, tiled=T...  29.3 us
  transfers between devices with their start and end apart: 4, of which 3 were waited for; matrix products, arithmetic and copies ran while one was open for 12% of the time, Pallas kernels for 0%

commit v1 on v0

--- a/solution.py
+++ b/solution.py
@@ -1,10 +1,210 @@
+import functools
+
 import jax
 import jax.numpy as jnp
 from jax import lax
+from jax.experimental import pallas as pl
+from jax.experimental.pallas import tpu as pltpu
 from jax.sharding import PartitionSpec as P
 
-
-def body(master_gate, master_up, master_down, router_weight, router_gain):
+MESH = pl.DeviceIdType.MESH
+LANES = 128
+PAIR = 2
+
+
+def kernel(
+    n, groups_of_experts, gate, up, down, weight, gain,
+    out_gate, out_up, out_down, scales, router,
+    wide_max, tall_max, wide, tall, turned, column, stage, local, got, kept, part, rows,
+    load_max, load_bulk, msg_send, msg_recv, bulk_send, bulk_recv, own_sem, router_sem,
+):
+    me = lax.axis_index("shard")
+    team = lax.axis_index("expert")
+    experts, depth, inner = gate.shape
+    block = inner // n
+    per_array = experts // PAIR
+    total = 3 * per_array
+    wide_groups = 2 * per_array
+    bits = n.bit_length() - 1
+    steps = bits + 1
+    ins, outs = (gate, up, down), (out_gate, out_up, out_down)
+    core = lax.rem(me, 2)
+
+    def partner(step):
+        size = 1 if step == steps - 1 else 2**step
+        return me + (1 - 2 * lax.rem(me // size, 2)) * size
+
+    barrier = pltpu.get_barrier_semaphore()
+    for d in range(1, n):
+        pl.semaphore_signal(barrier, inc=1, device_id={"shard": lax.rem(me + d, n)}, device_id_type=MESH)
+    for d in range(1, groups_of_experts):
+        pl.semaphore_signal(
+            barrier, inc=1, device_id={"expert": lax.rem(team + d, groups_of_experts)}, device_id_type=MESH
+        )
+
+    def load(group, wide_buf, tall_buf, sem, act):
+        for m in range(3):
+
+            @pl.when(group // per_array == m)
+            def _():
+                first = lax.rem(group, per_array) * PAIR
+                act(pltpu.make_async_copy(ins[m].at[pl.ds(first, PAIR)], tall_buf if m == 2 else wide_buf, sem))
+
+    load(0, wide_max, tall_max, load_max, lambda c: c.start())
+    load(0, wide, tall, load_bulk, lambda c: c.start())
+    pl.semaphore_wait(barrier, n + groups_of_experts - 2)
+
+    team_rows = pl.ds(pl.multiple_of(team * part.shape[0], part.shape[0]), part.shape[0])
+    my_columns = pl.ds(pl.multiple_of(me * depth, depth), depth)
+    product = (weight[...] * gain[...]).astype(jnp.bfloat16)
+    part[...] = product
+    rows[team_rows, my_columns] = product
+    for d in range(1, n):
+        pltpu.make_async_remote_copy(
+            part, rows.at[team_rows, my_columns], router_sem.at[0], router_sem.at[1],
+            device_id={"shard": lax.rem(me + d, n)}, device_id_type=MESH,
+        ).start()
+    router_bytes = rows.at[pl.ds(0, part.shape[0]), pl.ds(0, (n - 1) * depth)]
+    team_bytes = rows.at[pl.ds(0, (groups_of_experts - 1) * part.shape[0])]
+
+    def message(step, group):
+        source = local.at[group * PAIR + 1 - core] if step == 0 else kept.at[step, group]
+        return pltpu.make_async_remote_copy(
+            source, got.at[step, group], msg_send.at[step, group], msg_recv.at[step, group],
+            device_id={"shard": partner(step)}, device_id_type=MESH,
+        )
+
+    def local_max(group):
+        load(group, wide_max, tall_max, load_max, lambda c: c.wait())
+
+        @pl.when(group < wide_groups)
+        def _():
+            for j in range(PAIR):
+                for b in range(inner // LANES):
+                    lanes = pl.ds(b * LANES, LANES)
+                    local[group * PAIR + j, :, lanes] = jnp.max(jnp.abs(wide_max[j, :, lanes]), axis=0, keepdims=True)
+
+        @pl.when(group >= wide_groups)
+        def _():
+            for j in range(PAIR):
+                for b in range(inner // LANES):
+                    lanes = pl.ds(b * LANES, LANES)
+                    most = jnp.abs(tall_max[j, lanes, pl.ds(0, LANES)])
+                    for h in range(1, depth // LANES):
+                        most = jnp.maximum(most, jnp.abs(tall_max[j, lanes, pl.ds(h * LANES, LANES)]))
+                    local[group * PAIR + j, :, lanes] = jnp.max(most.T, axis=0, keepdims=True)
+
+        @pl.when(group + 1 < total)
+        def _():
+            load(group + 1, wide_max, tall_max, load_max, lambda c: c.start())
+
+        message(0, group).start()
+
+    def reduce_step(step, group):
+        message(step - 1, group).wait_recv()
+        held = local[group * PAIR + core] if step == 1 else kept[step - 1, group]
+        most = jnp.maximum(held, got[step - 1, group])
+        kept[step, group] = most
+        if step == steps - 1:
+            scales[group * PAIR + core] = most
+        message(step, group).start()
+
+    def normalise(j, source, chunk):
+        for p in range(n):
+            part_rows = pl.ds(p * block, block)
+            for h in range(depth // LANES):
+                lanes = pl.ds(h * LANES, LANES)
+                x = source[part_rows, lanes] if j is None else source[j, part_rows, lanes]
+                stage[chunk, p, :, lanes] = (x / column[part_rows]).astype(jnp.bfloat16)
+
+    def bulk(group):
+        message(steps - 1, group).wait_recv()
+        scales[group * PAIR + 1 - core] = got[steps - 1, group]
+        load(group, wide, tall, load_bulk, lambda c: c.wait())
+
+        @pl.loop(0, PAIR)
+        def _(j):
+            chunk = group * PAIR + j
+            for b in range(inner // LANES):
+                lanes = pl.ds(b * LANES, LANES)
+                column[lanes] = jnp.broadcast_to(scales[chunk, :, lanes], (LANES, LANES)).T
+
+            @pl.when(group < wide_groups)
+            def _():
+                for b in range(inner // LANES):
+                    lanes = pl.ds(b * LANES, LANES)
+                    for h in range(depth // LANES):
+                        half = pl.ds(h * LANES, LANES)
+                        turned[lanes, half] = wide[j, half, lanes].T
+                normalise(None, turned, chunk)
+
+            @pl.when(group >= wide_groups)
+            def _():
+                normalise(j, tall, chunk)
+
+            for m in range(3):
+
+                @pl.when(group // per_array == m)
+                def _():
+                    place = outs[m].at[chunk - m * experts, :, my_columns]
+                    for d in range(n):
+                        p = lax.rem(me + n // 2 + d, n)
+                        if d == n // 2:
+                            pltpu.make_async_copy(stage.at[chunk, me], place, own_sem.at[m]).start()
+                        else:
+                            pltpu.make_async_remote_copy(
+                                stage.at[chunk, p], place, bulk_send.at[m], bulk_recv.at[m],
+                                device_id={"shard": p}, device_id_type=MESH,
+                            ).start()
+
+        @pl.when(group + 1 < total)
+        def _():
+            load(group + 1, wide, tall, load_bulk, lambda c: c.start())
+
+    @pl.loop(0, total + steps)
+    def _(t):
+        for step in reversed(range(1, steps)):
+
+            @pl.when((t >= step) & (t < total + step))
+            def _():
+                reduce_step(step, t - step)
+
+        @pl.when(t < total)
+        def _():
+            local_max(t)
+
+        @pl.when(t == 1)
+        def _():
+            pltpu.make_async_copy(router_bytes, router_bytes, router_sem.at[1]).wait()
+            for d in range(1, groups_of_experts):
+                pltpu.make_async_remote_copy(
+                    rows.at[team_rows], rows.at[team_rows], router_sem.at[2], router_sem.at[3],
+                    device_id={"expert": lax.rem(team + d, groups_of_experts)}, device_id_type=MESH,
+                ).start()
+
+        @pl.when(t >= steps)
+        def _():
+            bulk(t - steps)
+
+    pltpu.make_async_copy(router_bytes, router_bytes, router_sem.at[0]).wait()
+    for s in (2, 3):
+        pltpu.make_async_copy(team_bytes, team_bytes, router_sem.at[s]).wait()
+    router[...] = rows[...]
+
+    @pl.loop(0, total)
+    def _(group):
+        for step in range(steps):
+            message(step, group).wait_send()
+
+    for m in range(3):
+        sent = outs[m].at[:, :, pl.ds(0, (n - 1) * depth)]
+        own = outs[m].at[:, :, pl.ds(0, depth)]
+        pltpu.make_async_copy(own, own, own_sem.at[m]).wait()
+        pltpu.make_async_copy(sent, sent, bulk_send.at[m]).wait()
+        pltpu.make_async_copy(sent, sent, bulk_recv.at[m]).wait()
+
+
+def plain(master_gate, master_up, master_down, router_weight, router_gain):
     scale_gate, scale_up, scale_down = lax.pmax(
         (
             jnp.max(jnp.abs(master_gate), axis=1),
@@ -39,6 +239,57 @@
 
 
 def solution(mesh):
+    n, teams = mesh.shape["shard"], mesh.shape["expert"]
+
+    def body(master_gate, master_up, master_down, router_weight, router_gain):
+        experts, depth, inner = master_gate.shape
+        block = inner // n
+        chunks = 3 * experts
+        groups = chunks // PAIR
+        steps = n.bit_length()
+        columns = router_weight.shape[1]
+        fits = depth % LANES == 0 and inner % LANES == 0 and block % 8 == 0
+        if n < 4 or n & (n - 1) or experts % PAIR or not fits:
+            return plain(master_gate, master_up, master_down, router_weight, router_gain)
+        f32, bf16 = jnp.float32, jnp.bfloat16
+        dma = pltpu.SemaphoreType.DMA
+        final = jax.ShapeDtypeStruct((experts, block, n * depth), bf16)
+        hbm, vmem = pl.BlockSpec(memory_space=pl.ANY), pl.BlockSpec(memory_space=pltpu.VMEM)
+        gate, up, down, scales, router = pl.pallas_call(
+            functools.partial(kernel, n, teams),
+            out_shape=(
+                final, final, final,
+                jax.ShapeDtypeStruct((chunks, 1, inner), f32),
+                jax.ShapeDtypeStruct((teams * columns, n * depth), bf16),
+            ),
+            in_specs=[hbm, hbm, hbm, vmem, vmem],
+            out_specs=(hbm, hbm, hbm, vmem, vmem),
+            scratch_shapes=[
+                pltpu.VMEM((PAIR, depth, inner), f32),
+                pltpu.VMEM((PAIR, inner, depth), f32),
+                pltpu.VMEM((PAIR, depth, inner), f32),
+                pltpu.VMEM((PAIR, inner, depth), f32),
+                pltpu.VMEM((inner, depth), f32),
+                pltpu.VMEM((inner, LANES), f32),
+                pltpu.VMEM((chunks, n, block, depth), bf16),
+                pltpu.VMEM((chunks, 1, inner), f32),
+                pltpu.VMEM((steps, groups, 1, inner), f32),
+                pltpu.VMEM((steps, groups, 1, inner), f32),
+                pltpu.VMEM((columns, depth), bf16),
+                pltpu.VMEM((teams * columns, n * depth), bf16),
+                dma, dma,
+                dma((steps, groups)), dma((steps, groups)),
+                dma((3,)), dma((3,)), dma((3,)), dma((4,)),
+            ],
+            compiler_params=pltpu.CompilerParams(
+                collective_id=0, has_side_effects=True, vmem_limit_bytes=62 * 1024 * 1024
+            ),
+        )(master_gate, master_up, master_down, router_weight.T, router_gain[None, :])
+        mine = lax.dynamic_slice_in_dim(
+            scales.reshape(3, experts, inner), lax.axis_index("shard") * block, block, axis=2
+        )
+        return (gate.swapaxes(1, 2), up.swapaxes(1, 2), down, mine[0], mine[1], mine[2], router.T)
+
     return jax.shard_map(
         body,
         mesh=mesh,

time: 988 us -> 793 us (0.80)
  Pallas kernels: 0 us -> 766 us
  waiting for transfers between devices: 464 us -> 0 us
  blocking collectives: 266 us -> 0 us
  local copies, waits for them, and re-layouts: 140 us -> 26.4 us
  other arithmetic: 84.8 us -> 0.01 us
  starting transfers between devices: 16 us -> 0 us
  between operations: 14.2 us -> 0.66 us
    pallas_call x0 -> x1, Pallas kernels: none -> 766 us  [body(): pl.pallas_call(functools.partial(kernel, n, teams), out_shape=(final, fin...]
    all_to_all x3 -> x0, waiting for transfers between devices: 432 us -> none  [the longest x1 218 us: body(): lax.all_to_all(narrow_up, 'shard', split_axis=2, concat_axis=1, tiled=True)]
    all_gather x2 -> x0, blocking collectives: 266 us -> none  [the longest x1 257 us: body(): row_router = lax.all_gather(part_router, 'shard', axis=0, tiled=True)]
    all_to_all x6 -> x0, local copies, waits for them, and re-layouts: 87.9 us -> none  [the longest x2 29.3 us: body(): lax.all_to_all(narrow_down, 'shard', split_axis=1, concat_axis=2, tiled=T...]
    convert_element_type x4 -> x0, other arithmetic: 61.1 us -> none  [the longest x1 32.6 us: body(): (master_down / jnp.expand_dims(scale_down, 2)).astype(jnp.bfloat16)]
    pmax x1 -> x0, waiting for transfers between devices: 32.5 us -> none  [body(): lax.pmax((jnp.max(jnp.abs(master_gate), axis=1), jnp.max(jnp.abs(master_u...]
    reduce_max x3 -> x0, other arithmetic: 23.7 us -> none  [the longest x1 10.8 us: body(): jnp.max(jnp.abs(master_up), axis=1)]
    unnamed x23 -> x15, local copies, waits for them, and re-layouts: 48.2 us -> 25.7 us
  transfers between devices with their start and end apart: 4 -> 0, of which waited for: 3 -> 0; matrix products, arithmetic and copies ran while one was open for 12% -> 0% of each run, Pallas kernels for 0% -> 0%
where the time goes in v1:
time: 793 us
  Pallas kernels  766 us (97%)
  local copies, waits for them, and re-layouts  26.4 us (3%)
    pallas_call x1, Pallas kernels, body(): pl.pallas_call(functools.partial(kernel, n, teams), out_shape=(final, fin...  766 us
    unnamed x15, local copies, waits for them, and re-layouts  25.7 us

profile of v1, /device:TPU:0, one launch (start us, length us, event | category | flops | bytes accessed | tf_op | source)
XLA Modules:
  0.0 793.1 jit_solution(17037276164366188370)
XLA Ops:
  0.6 766.1 %shard_map.108 = (bf16[16,176,2048]{2,1,0:T(8,128)(2,1)}, bf16[16,176,2048]{2,1,0:T(8,128)(2,1)}, bf16[16,176,2048]{2,1,0:T(8,128)(2,1)}, f32[48,1,1408]{2,1,0:T(1,128)}, bf16[64,2048]{1,0:T(8,128)(2,1)}) custom-call(f32[16,256,1408]{2,1,0:T(8,128)} %gate.1, f32[16,256,1408]{2,1,0:T(8,128)} %up.1, f32[16,1408,256]{2,1,0:T(8,128)} %down.1, ...), custom_call_target="tpu_custom_call" | custom-call | tf_op jit(solution)/shard_map/pallas_call | solution.py:258
  766.7 1.0 copy.12
  767.7 0.7 dynamic-slice_bitcast_fusion
  768.4 0.0 copy-start
  768.4 0.0 slice-start
  768.4 0.0 slice-start.1
  768.4 12.0 %copy.17 = bf16[16,2048,176]{1,2,0:T(8,128)(2,1)} copy(bf16[16,2048,176]{1,2,0:T(8,128)(2,1)} %bitcast.15) | data formatting | bytes 23068672
  780.4 0.0 copy-done
  780.4 0.0 slice-start.2
  780.4 5.8 copy.18
  786.2 0.0 slice-done
  786.2 0.0 slice-done.1
  786.2 1.7 slice-done.2
  788.0 0.0 copy-start.1
  788.0 4.4 copy.19
  792.4 0.0 copy-done.1
  792.4 0.7 copy.20
  (1 shorter events, 0.0 us)
Async XLA Ops:
  768.4 12.0 %copy-start = (bf16[16,176,2048]{2,1,0:T(8,128)(2,1)S(1)}, bf16[16,176,2048]{2,1,0:T(8,128)(2,1)}, u32[]{:S(2)}) copy-start(bf16[16,176,2048]{2,1,0:T(8,128)(2,1)} %get-tuple-element.13) | copy-start | bytes 34603012
  768.4 17.8 %slice-start = ((s8[11534336]{0:T(1024)(128)(4,1)}), s8[4194304]{0:T(1024)(128)(4,1)S(1)}, s32[]{:S(2)}) async-start(s8[11534336]{0:T(1024)(128)(4,1)} %bitcast.12), calls=%async_computation | async-start | bytes 8388608
  768.4 17.8 %slice-start.1 = ((s8[11534336]{0:T(1024)(128)(4,1)}), s8[4194304]{0:T(1024)(128)(4,1)S(1)}, s32[]{:S(2)}) async-start(s8[11534336]{0:T(1024)(128)(4,1)} %bitcast.12), calls=%async_computation.1 | async-start | bytes 8388608
  780.4 7.6 slice-start.2
  788.0 4.4 copy-start.1
